TPU v7x, 32 devices: a whole 2x2x4 slice. The times are simulated.
32 devices in a mesh: chan: 4 (over y, x), tm: 8 (over z, core).
Axes of the slice: x: 2, y: 2, z: 4, core: 2. Of those that a mesh axis runs over, the one named last changes fastest.
Arguments:
- strain: float32 [768, 131072], P('chan', 'tm'), may hold values from -6 to 6
Outputs:
- power: float32 [768, 8192], P('chan', 'tm')
- nyquist: float32 [768], P('chan')
- mean_power: float32 [8192], P('tm')
All inputs are finite; a program needn't handle non-finite values.
Results may differ from a plain program's by a relative error of at most 0.00007.
Values sent between devices are 32-bit elements; how exact they have to be, the bound alone decides.
A program may use at most 192 MiB of HBM per device.

v0:
```python
import jax
import jax.numpy as jnp
from jax import lax
from jax.sharding import PartitionSpec as P

ROOT = 128


highest_mode = lax.Precision.HIGHEST


def shifted(block, axis, distance):
    devices = range(lax.axis_size(axis))
    route = [(i - distance, i) for i in devices if i - distance in devices]
    return lax.ppermute(block, axis, route)


def hann_window(seg_len):
    sample_pos = jnp.arange(seg_len, dtype=jnp.float32)
    return 0.5 - 0.5 * jnp.cos(2.0 * jnp.pi * sample_pos / seg_len)


def dft_tables(root_len):
    positions = jnp.arange(root_len, dtype=jnp.int32)
    products = positions[:, None] * positions[None, :]
    short_angle = 2.0 * jnp.pi * (products % root_len).astype(jnp.float32) / root_len
    long_angle = 2.0 * jnp.pi * products.astype(jnp.float32) / (root_len * root_len)
    half_root = root_len // 2
    parity = (1 - 2 * (positions % 2)).astype(jnp.float32)
    return (
        jnp.cos(short_angle),
        jnp.sin(short_angle),
        jnp.cos(long_angle),
        jnp.sin(long_angle),
        jnp.cos(short_angle[:half_root]),
        jnp.sin(short_angle[:half_root]),
        parity,
    )


def periodogram(pieces, tables, window):
    cos_short, sin_short, cos_long, sin_long, cos_half, sin_half, parity = tables
    root_len = cos_short.shape[0]
    piece_rows = pieces.shape[0]
    centred = (pieces - jnp.mean(pieces, axis=1, keepdims=True)) * window
    folded = centred.reshape(piece_rows, root_len, root_len)
    real_first = jnp.einsum("ka,rab->rkb", cos_short, folded, precision=highest_mode)
    imag_first = -jnp.einsum("ka,rab->rkb", sin_short, folded, precision=highest_mode)
    real_twist = real_first * cos_long + imag_first * sin_long
    imag_twist = imag_first * cos_long - real_first * sin_long
    real_final = jnp.einsum(
        "rkb,qb->rqk", real_twist, cos_half, precision=highest_mode
    ) + jnp.einsum("rkb,qb->rqk", imag_twist, sin_half, precision=highest_mode)
    imag_final = jnp.einsum(
        "rkb,qb->rqk", imag_twist, cos_half, precision=highest_mode
    ) - jnp.einsum("rkb,qb->rqk", real_twist, sin_half, precision=highest_mode)
    spectrum_power = (real_final * real_final + imag_final * imag_final).reshape(piece_rows, -1)
    edge_term = jnp.sum(folded * parity, axis=(1, 2))
    return (spectrum_power, edge_term * edge_term)


def per_device(strain):
    chan_rows, time_width = strain.shape
    seg_len = ROOT * ROOT
    half_len = seg_len // 2
    window = hann_window(seg_len)
    energy = jnp.sum(window * window)
    tables = dft_tables(ROOT)
    tm_count = lax.axis_size("tm")
    block_count = time_width // half_len
    segments = block_count * tm_count - 1
    band_width = half_len // tm_count
    follower = shifted(strain[:, :half_len], "tm", -1)
    extended = jnp.concatenate([strain, follower], axis=1)
    is_last = (lax.axis_index("tm") == tm_count - 1).astype(jnp.float32)
    running_total = jnp.zeros((chan_rows, half_len), jnp.float32)
    nyquist_part = jnp.zeros((chan_rows,), jnp.float32)
    for segment_index in range(block_count):
        start = segment_index * half_len
        spectrum_power, edge_term = periodogram(
            extended[:, start : start + seg_len], tables, window
        )
        if segment_index == block_count - 1:
            keep_factor = 1.0 - is_last
            spectrum_power = spectrum_power * keep_factor
            edge_term = edge_term * keep_factor
        running_total = running_total + spectrum_power
        nyquist_part = nyquist_part + edge_term
    band_total = lax.psum_scatter(running_total, "tm", scatter_dimension=1, tiled=True)
    edges_total = lax.psum(nyquist_part, "tm")
    bin_index = lax.axis_index("tm") * band_width + jnp.arange(band_width, dtype=jnp.int32)
    doubling = jnp.where(bin_index == 0, 1.0, 2.0).astype(jnp.float32)
    power = band_total * doubling / (segments * energy)
    nyquist = edges_total / (segments * energy)
    channel_sum = lax.psum(jnp.sum(power, axis=0), "chan")
    mean_power = channel_sum / (chan_rows * lax.axis_size("chan"))
    return (power, nyquist, mean_power)


def solution(mesh):
    in_specs = (P("chan", "tm"),)
    out_specs = (P("chan", "tm"), P("chan"), P("tm"))
    return jax.shard_map(
        per_device, mesh=mesh, in_specs=in_specs, out_specs=out_specs, check_vma=False
    )
```

profile of v0, /device:TPU:0, one launch (start us, length us, event | category | flops | bytes accessed | tf_op | source)
XLA Modules:
  0.0 459.2 jit_solution(7890013996807659785)
XLA Ops:
  7.2 0.0 reduce-scatter.2.cloned.1.call-start
  7.2 6.1 %slice.25 = f32[192,8192]{1,0:T(8,128)} slice(f32[192,16384]{1,0:T(8,128)} %param.1), slice={[0:192], [0:8192]} | slice | bytes 12582912 | tf_op jit(solution)/shard_map/slice | solution.py:73
  13.3 1.3 collective-permute-start
  14.6 0.2 fusion.37
  14.8 0.1 copy.5
  14.9 0.2 fusion.36
  15.1 0.1 copy.7
  15.3 0.2 multiply_subtract_fusion
  15.6 10.1 %collective-permute-done = f32[192,8192]{1,0:T(8,128)} collective-permute-done((f32[192,8192]{1,0:T(8,128)}, f32[192,8192]{1,0:T(8,128)}, u32[]{:S(2)}, u32[]{:S(2)}) %collective-permute-start) | collective-permute-done | bytes 6291488 | tf_op jit(solution)/shard_map/ppermute | solution.py:15
  25.6 9.8 %fusion.75 = (f32[192]{0:T(256)S(1)}, f32[192]{0:T(256)S(1)}) fusion(f32[192,16384]{1,0:T(8,128)} %param.1, f32[192,8192]{1,0:T(8,128)} %collective-permute-done), kind=kLoop, calls=%fused_computation.94 | loop fusion | flops 9436800 | bytes 18875904 | tf_op jit(solution)/shard_map/reduce_sum | solution.py:45
  35.5 22.8 %multiply_reduce_fusion.1 = (f32[192]{0:T(256)S(1)}, f32[192]{0:T(256)S(1)}, f32[24,8,128,128]{3,1,2,0:T(8,128)}, f32[24,8,128,128]{3,1,2,0:T(8,128)}) fusion(f32[192,16384]{1,0:T(8,128)} %param.1, f32[16384]{0:T(1024)S(1)} %broadcast_bitcast_fusion, f32[16384]{0:T(1024)S(1)} %multiply_subtract_fusion, f32[192]{0:T(256)S(1)} %get-tuple-element.12, ...), kind=kLoop, calls=%fused_computation.14 | loop fusion | flops 28311168 | bytes 44174336 | tf_op jit(solution)/shard_map/reduce_sum | solution.py:58
  58.3 11.5 %copy.30 = f32[24,8,128,128]{3,2,1,0:T(8,128)} copy(f32[24,8,128,128]{3,1,2,0:T(8,128)} %get-tuple-element.10) | data formatting | bytes 25165824
  69.8 0.0 slice-start
  69.8 0.0 slice-start.1
  69.8 0.0 slice-start.2
  69.8 24.5 %fusion.30 = f32[192,128,128]{2,1,0:T(8,128)S(1)} fusion(f32[192,128,128]{2,1,0:T(8,128)} %bitcast.93), kind=kOutput, calls=%fused_computation.39 | convolution fusion | flops 4832067584 | bytes 25165824 | tf_op jit(solution)/shard_map/ka,rab->rkb/dot_general | solution.py:48
  94.3 0.0 slice-done
  94.3 0.0 slice-done.1
  94.4 0.0 slice-done.2
  94.4 23.6 %fusion.34 = f32[192,128,128]{2,1,0:T(8,128)} fusion(f32[192,128,128]{2,1,0:T(8,128)S(1)} %bitcast.96), kind=kOutput, calls=%fused_computation.43 | convolution fusion | flops 4832067584 | bytes 25165824 | tf_op jit(solution)/shard_map/ka,rab->rkb/dot_general | solution.py:47
  117.9 13.1 %fusion.10 = f32[64,192,128]{2,0,1:T(8,128)} fusion(f32[192,128,128]{2,1,0:T(8,128)} %fusion.34, f32[192,128,128]{2,1,0:T(8,128)S(1)} %fusion.30, f32[128,128]{0,1:T(8,128)S(1)} %copy.7, f32[128,128]{0,1:T(8,128)S(1)} %copy.5, f32[128,128]{1,0:T(8,128)S(1)} %fusion.27), kind=kOutput, calls=%fused_computation.23 | convolution fusion | flops 2428502016 | bytes 31621120 | tf_op jit(solution)/shard_map/rkb,qb->rqk/dot_general | solution.py:56
  131.1 13.2 %fusion.12 = f32[64,192,128]{2,0,1:T(8,128)} fusion(f32[192,128,128]{2,1,0:T(8,128)} %fusion.34, f32[192,128,128]{2,1,0:T(8,128)S(1)} %fusion.30, f32[128,128]{0,1:T(8,128)S(1)} %copy.7, f32[128,128]{0,1:T(8,128)S(1)} %copy.5, f32[128,128]{1,0:T(8,128)S(1)} %fusion.27), kind=kOutput, calls=%fused_computation.24 | convolution fusion | flops 2428502016 | bytes 31621120 | tf_op jit(solution)/shard_map/rkb,qb->rqk/dot_general | solution.py:51
  144.3 12.9 %fusion.6 = f32[64,192,128]{2,0,1:T(8,128)} fusion(f32[192,128,128]{2,1,0:T(8,128)} %fusion.34, f32[192,128,128]{2,1,0:T(8,128)S(1)} %fusion.30, f32[128,128]{0,1:T(8,128)S(1)} %copy.7, f32[128,128]{0,1:T(8,128)S(1)} %copy.5, f32[128,128]{1,0:T(8,128)S(1)} %fusion.27), kind=kOutput, calls=%fused_computation.21 | convolution fusion | flops 2428502016 | bytes 31621120 | tf_op jit(solution)/shard_map/rkb,qb->rqk/dot_general | solution.py:54
  157.2 12.9 %fusion.8 = f32[64,192,128]{2,0,1:T(8,128)} fusion(f32[192,128,128]{2,1,0:T(8,128)} %fusion.34, f32[192,128,128]{2,1,0:T(8,128)S(1)} %fusion.30, f32[128,128]{0,1:T(8,128)S(1)} %copy.7, f32[128,128]{0,1:T(8,128)S(1)} %copy.5, f32[128,128]{1,0:T(8,128)S(1)} %fusion.27), kind=kOutput, calls=%fused_computation.22 | convolution fusion | flops 2428502016 | bytes 31621120 | tf_op jit(solution)/shard_map/rkb,qb->rqk/dot_general | solution.py:53
  170.1 11.4 %copy.31 = f32[24,8,128,128]{3,2,1,0:T(8,128)} copy(f32[24,8,128,128]{3,1,2,0:T(8,128)} %get-tuple-element.9) | data formatting | bytes 25165824
  181.5 0.0 slice-start.3
  181.5 0.0 slice-start.4
  181.5 0.0 slice-start.5
  181.5 24.7 %fusion.28 = f32[192,128,128]{2,1,0:T(8,128)S(1)} fusion(f32[192,128,128]{2,1,0:T(8,128)} %bitcast.97), kind=kOutput, calls=%fused_computation.37 | convolution fusion | flops 4832067584 | bytes 25165824 | tf_op jit(solution)/shard_map/ka,rab->rkb/dot_general | solution.py:48
  206.2 0.0 slice-done.3
  206.2 0.0 slice-done.4
  206.2 0.0 slice-done.5
  206.2 0.0 copy-start
  206.3 23.5 %fusion.32 = f32[192,128,128]{2,1,0:T(8,128)} fusion(f32[192,128,128]{2,1,0:T(8,128)S(1)} %bitcast.100), kind=kOutput, calls=%fused_computation.41 | convolution fusion | flops 4832067584 | bytes 25165824 | tf_op jit(solution)/shard_map/ka,rab->rkb/dot_general | solution.py:47
  229.8 12.8 %fusion.16 = f32[64,192,128]{2,0,1:T(8,128)} fusion(f32[192,128,128]{2,1,0:T(8,128)} %fusion.32, f32[192,128,128]{2,1,0:T(8,128)S(1)} %fusion.28, f32[128,128]{0,1:T(8,128)S(1)} %copy.7, f32[128,128]{0,1:T(8,128)S(1)} %copy.5, f32[128,128]{1,0:T(8,128)S(1)} %fusion.27), kind=kOutput, calls=%fused_computation.26 | convolution fusion | flops 2428502016 | bytes 31621120 | tf_op jit(solution)/shard_map/rkb,qb->rqk/dot_general | solution.py:53
  242.6 13.3 %fusion.18 = f32[64,192,128]{2,0,1:T(8,128)} fusion(f32[192,128,128]{2,1,0:T(8,128)} %fusion.32, f32[192,128,128]{2,1,0:T(8,128)S(1)} %fusion.28, f32[128,128]{0,1:T(8,128)S(1)} %copy.7, f32[128,128]{0,1:T(8,128)S(1)} %copy.5, f32[128,128]{1,0:T(8,128)S(1)} %fusion.27), kind=kOutput, calls=%fused_computation.27 | convolution fusion | flops 2428502016 | bytes 31621120 | tf_op jit(solution)/shard_map/rkb,qb->rqk/dot_general | solution.py:56
  255.9 0.0 copy-done
  255.9 12.9 %fusion.14 = f32[64,192,128]{2,0,1:T(8,128)} fusion(f32[192,128,128]{2,1,0:T(8,128)} %fusion.32, f32[192,128,128]{2,1,0:T(8,128)S(1)} %fusion.28, f32[128,128]{0,1:T(8,128)S(1)} %copy.7, f32[128,128]{0,1:T(8,128)S(1)} %copy.5, f32[128,128]{1,0:T(8,128)S(1)} %fusion.27), kind=kOutput, calls=%fused_computation.25 | convolution fusion | flops 2428502016 | bytes 31621120 | tf_op jit(solution)/shard_map/rkb,qb->rqk/dot_general | solution.py:54
  268.8 28.2 %multiply_add_fusion = f32[64,192,128]{2,0,1:T(8,128)} fusion(f32[64,192,128]{2,0,1:T(8,128)} %fusion.14, f32[64,192,128]{2,0,1:T(8,128)} %fusion.18, f32[64,192,128]{2,0,1:T(8,128)} %fusion.16, f32[64,192,128]{2,0,1:T(8,128)} %fusion.6, f32[64,192,128]{2,0,1:T(8,128)} %fusion.10, f32[64,192,128]{2,0,1:T(8,128)} %fusion.12, f32[64,192,128]{2,0,1:T(8,128)} %fusion.8, ...), kind=kOutput, calls=%fused_computation.20 | convolution fusion | flops 2447376384 | bytes 75661312 | tf_op jit(solution)/shard_map/rkb,qb->rqk/dot_general | solution.py:51
  297.0 10.9 %copy.34 = f32[24,8,64,128]{3,1,2,0:T(8,128)} copy(f32[24,8,64,128]{3,2,1,0:T(8,128)} %bitcast.102) | data formatting | bytes 12582912
  308.0 0.0 reduce-scatter.2.cloned.1.call-update
  308.0 0.8 multiply_reduce_fusion.2
  309.5 75.8 %psum.14 = f32[192]{0:T(256)S(1)} all-reduce(f32[192]{0:T(256)S(1)} %multiply_add_fusion.1), channel_id=1, replica_groups=mesh['chan'=4,'tm'=8] {'tm'}, use_global_device_ids=true, to_apply=%region_6.7 | all-reduce | flops 192 | bytes 1536 | tf_op jit(solution)/shard_map/psum | solution.py:90
  385.3 0.6 broadcast_divide_fusion
  385.9 53.7 %reduce-scatter.2.cloned.1.call-done = f32[192,1024]{1,0:T(8,128)} async-done(((f32[192,8192]{1,0:T(8,128)}), f32[192,1024]{1,0:T(8,128)}) %reduce-scatter.2.cloned.1.call-update) | async-done | bytes 786448 | tf_op jit(solution)/shard_map/reduce_scatter | solution.py:89
  439.5 2.1 fusion.76
  441.6 9.8 %psum.15 = f32[1024]{0:T(1024)S(1)} all-reduce(f32[1024]{0:T(1024)S(1)} %get-tuple-element.7), channel_id=1, replica_groups=mesh['chan'=4,'tm'=8] {'chan'}, use_global_device_ids=true, to_apply=%region_8.9 | all-reduce | flops 1024 | bytes 8192 | tf_op jit(solution)/shard_map/psum | solution.py:95
  451.5 0.6 broadcast_multiply_fusion
  (8 shorter events, 0.1 us)
Async XLA Ops:
  7.2 432.4 %reduce-scatter.2.cloned.1.call-start = ((), (), s32[]{:S(2)}) async-start(), calls=%async_computation.1 | async-start | bytes 7077888 | tf_op jit(solution)/shard_map/reduce_scatter | solution.py:89
  13.3 12.4 %collective-permute-start = (f32[192,8192]{1,0:T(8,128)}, f32[192,8192]{1,0:T(8,128)}, u32[]{:S(2)}, u32[]{:S(2)}) collective-permute-start(f32[192,8192]{1,0:T(8,128)} %slice.25), channel_id=1, source_target_pairs={{1,0},{2,1},{3,2},{4,3},{5,4},{6,5},{7,6},{9,8},{10,9},{11,10},{12... | collective-permute-start | bytes 18874376 | tf_op jit(solution)/shard_map/ppermute | solution.py:15
  69.8 24.5 %slice-start = ((s8[12582912]{0:T(1024)(128)(4,1)}), s8[4194304]{0:T(1024)(128)(4,1)S(1)}, s32[]{:S(2)}) async-start(s8[12582912]{0:T(1024)(128)(4,1)} %bitcast.94), calls=%async_computation.2 | async-start | bytes 8388608
  69.8 24.5 %slice-start.1 = ((s8[12582912]{0:T(1024)(128)(4,1)}), s8[4194304]{0:T(1024)(128)(4,1)S(1)}, s32[]{:S(2)}) async-start(s8[12582912]{0:T(1024)(128)(4,1)} %bitcast.94), calls=%async_computation.3 | async-start | bytes 8388608
  69.8 24.6 %slice-start.2 = ((s8[12582912]{0:T(1024)(128)(4,1)}), s8[4194304]{0:T(1024)(128)(4,1)S(1)}, s32[]{:S(2)}) async-start(s8[12582912]{0:T(1024)(128)(4,1)} %bitcast.94), calls=%async_computation.4 | async-start | bytes 8388608
  181.5 24.7 %slice-start.3 = ((s8[12582912]{0:T(1024)(128)(4,1)}), s8[4194304]{0:T(1024)(128)(4,1)S(1)}, s32[]{:S(2)}) async-start(s8[12582912]{0:T(1024)(128)(4,1)} %bitcast.98), calls=%async_computation.5 | async-start | bytes 8388608
  181.5 24.7 %slice-start.4 = ((s8[12582912]{0:T(1024)(128)(4,1)}), s8[4194304]{0:T(1024)(128)(4,1)S(1)}, s32[]{:S(2)}) async-start(s8[12582912]{0:T(1024)(128)(4,1)} %bitcast.98), calls=%async_computation.6 | async-start | bytes 8388608
  181.5 24.7 %slice-start.5 = ((s8[12582912]{0:T(1024)(128)(4,1)}), s8[4194304]{0:T(1024)(128)(4,1)S(1)}, s32[]{:S(2)}) async-start(s8[12582912]{0:T(1024)(128)(4,1)} %bitcast.98), calls=%async_computation.7 | async-start | bytes 8388608
  206.2 49.6 %copy-start = (f32[192,128,128]{2,1,0:T(8,128)}, f32[192,128,128]{2,1,0:T(8,128)S(1)}, u32[]{:S(2)}) copy-start(f32[192,128,128]{2,1,0:T(8,128)S(1)} %fusion.28) | copy-start | bytes 37748740
Sparse Core Ops, SparseCore 0:
  308.1 131.3 reduce-scatter.1
where the time goes:
time: 466 us; the launch traced here: 459 us
  matrix products  216 us (46%)
  blocking collectives  85.6 us (18%)
  waiting for transfers between devices  63.8 us (14%)
  local copies, waits for them, and re-layouts  40.1 us (9%)
  other arithmetic  37.6 us (8%)
  between operations  15.1 us (3%)
    psum x1, blocking collectives, per_device(): edges_total = lax.psum(nyquist_part, 'tm')  75.8 us
    reduce_scatter x1, waiting for transfers between devices, per_device(): lax.psum_scatter(running_total, 'tm', scatter_dimension=1, tiled=True)  53.7 us
    dot_general x2, matrix products, periodogram(): jnp.einsum('ka,rab->rkb', sin_short, folded, precision=highest_mode)  49.2 us
    dot_general x2, matrix products, periodogram(): jnp.einsum('ka,rab->rkb', cos_short, folded, precision=highest_mode)  47.1 us
    dot_general x2, matrix products, periodogram(): jnp.einsum('rkb,qb->rqk', real_twist, cos_half, precision=highest_mode)  41.5 us
    unnamed x17, local copies, waits for them, and re-layouts  33.8 us
    dot_general x2, matrix products, periodogram(): jnp.einsum('rkb,qb->rqk', real_twist, sin_half, precision=highest_mode)  26.4 us
    dot_general x2, matrix products, periodogram(): jnp.einsum('rkb,qb->rqk', imag_twist, cos_half, precision=highest_mode)  25.8 us
  transfers between devices with their start and end apart: 2, of which 2 were waited for; matrix products, arithmetic and copies ran while one was open for 1% of the time, Pallas kernels for 0%

commit v1 on v0

v1 whole, which is shorter than its diff:
```python
import functools

import jax
import jax.numpy as jnp
import numpy as np
from jax import lax
from jax.experimental import pallas as pl
from jax.experimental.pallas import tpu as pltpu
from jax.sharding import PartitionSpec as P

ROOT = 128
HALF = ROOT // 2
ROWS = 8


def split_np(table):
    table = table.astype(np.float32)
    high = table.astype(jnp.bfloat16)
    low = (table - high.astype(np.float32)).astype(jnp.bfloat16)
    return high, low


@functools.cache
def tables(tm_count):
    pos = np.arange(ROOT)
    short = 2.0 * np.pi * (np.outer(pos, pos) % ROOT) / ROOT
    cos_s, sin_s = np.cos(short), np.sin(short)
    first = np.concatenate([cos_s[:HALF], -sin_s[:HALF]], axis=0)
    first_hi, first_lo = split_np(first)
    first_all = np.concatenate(
        [
            np.concatenate([first_hi, first_hi], axis=1),
            np.concatenate([first_lo, first_lo], axis=1),
        ],
        axis=0,
    )
    bands = np.arange(HALF).reshape(tm_count, HALF // tm_count)
    order = np.concatenate([bands, ROOT - 1 - bands], axis=1).reshape(-1)
    cos_o, sin_o = cos_s[:, order], sin_s[:, order]
    second = np.concatenate(
        [np.concatenate([cos_o, -sin_o], axis=1), np.concatenate([sin_o, cos_o], axis=1)], axis=0
    )
    second_hi, second_lo = split_np(second)
    second_all = np.concatenate([second_hi, second_hi, second_lo], axis=0)
    long = 2.0 * np.pi * np.outer(np.arange(HALF + ROWS), pos) / (ROOT * ROOT)
    twist = np.concatenate([np.cos(long), np.sin(long)], axis=1).astype(np.float32)
    seg_len = ROOT * ROOT
    window = 0.5 - 0.5 * np.cos(2.0 * np.pi * np.arange(seg_len) / seg_len)
    energy = float(np.sum(window * window))
    return first_all, second_all, twist, window.reshape(ROOT, ROOT).astype(np.float32), energy


def split(value):
    high = value.astype(jnp.bfloat16)
    low = (value - high.astype(jnp.float32)).astype(jnp.bfloat16)
    return high, low


def stage_one(parts, window_ref, first_ref, twist_ref, buf, zbuf, ebuf, row, erow):
    half_len = ROOT * HALF
    total = jnp.zeros((ROWS, ROOT), jnp.float32)
    for ref, offset in parts:
        total = total + jnp.sum(
            jnp.stack([ref[:, offset + ROOT * a : offset + ROOT * (a + 1)] for a in range(HALF)]), axis=0
        )
    mean = jnp.sum(total, axis=1, keepdims=True) * (1.0 / (2 * half_len))
    mean = jnp.broadcast_to(mean, (ROWS, ROOT))
    even = jnp.zeros((ROWS, ROOT), jnp.float32)
    odd = jnp.zeros((ROWS, ROOT), jnp.float32)
    for a in range(ROOT):
        ref, offset = parts[a // HALF]
        start = offset + ROOT * (a % HALF)
        tile = (ref[:, start : start + ROOT] - mean) * window_ref[a : a + 1, :]
        buf[ROWS * a : ROWS * (a + 1), :] = tile
        if a % 2 == 0:
            even = even + tile
        else:
            odd = odd + tile
    alt = even - odd
    sign = (1 - 2 * (lax.broadcasted_iota(jnp.int32, (ROWS, ROOT), 1) % 2)).astype(jnp.float32)
    edge = jnp.sum((even + odd) * sign, axis=1, keepdims=True)
    turn = twist_ref[HALF : HALF + 1, :]
    high, low = split(jnp.concatenate([alt * turn[:, :ROOT], -alt * turn[:, ROOT:]], axis=1))
    ebuf[erow : erow + ROWS, :] = jnp.concatenate([high, low, high], axis=1)
    cos_t, sin_t = twist_ref[:HALF, :ROOT], twist_ref[:HALF, ROOT:]
    for r in range(0, ROWS, 2):
        pair = jnp.concatenate(
            [buf[pl.ds(r, ROOT, stride=ROWS), :], buf[pl.ds(r + 1, ROOT, stride=ROWS), :]], axis=1
        )
        high, low = split(pair)
        out = jnp.dot(
            first_ref[...], jnp.concatenate([high, low], axis=0), preferred_element_type=jnp.float32
        )
        out = out[:ROOT] + out[ROOT:]
        for s in range(2):
            re = out[:HALF, s * ROOT : (s + 1) * ROOT]
            im = out[HALF:, s * ROOT : (s + 1) * ROOT]
            z_hi, z_lo = split(
                jnp.concatenate([re * cos_t + im * sin_t, im * cos_t - re * sin_t], axis=1)
            )
            at = row + (r + s) * HALF
            zbuf[at : at + HALF, 0 : 2 * ROOT] = z_hi
            zbuf[at : at + HALF, 2 * ROOT : 4 * ROOT] = z_lo
            zbuf[at : at + HALF, 4 * ROOT :] = z_hi
    return edge * edge


def squares(left, right):
    out = jnp.dot(left, right, preferred_element_type=jnp.float32)
    return out[:, :ROOT] * out[:, :ROOT] + out[:, ROOT:] * out[:, ROOT:]


def group_sums(lo_ref, hi_ref, right_ref, left_ref, right_on, left_on, per_dev, consts, scratch, put, put_edge):
    window_ref, first_ref, second_ref, twist_ref = consts
    buf, zbuf, ebuf, psum = scratch
    half_len = ROOT * HALF
    block = ROWS * HALF
    lane = lax.broadcasted_iota(jnp.int32, (ROWS, ROOT), 1)
    nyq = []
    for side, own, other, on in ((0, lo_ref, right_ref, right_on), (1, hi_ref, left_ref, left_on)):
        straddle = ((own, half_len), (other, 0)) if side == 0 else ((other, 0), (own, 0))
        first = stage_one(
            ((own, 0), (own, half_len)), window_ref, first_ref, twist_ref, buf, zbuf, ebuf, 0, side * 2 * ROWS
        )
        second = stage_one(
            straddle, window_ref, first_ref, twist_ref, buf, zbuf, ebuf, block, (side * 2 + 1) * ROWS
        )
        nyq.append(first + on * second)
        for r in range(ROWS):
            rows = pl.ds(r * HALF, HALF)
            both = jnp.concatenate([zbuf[rows, :], zbuf[pl.ds(block + r * HALF, HALF), :]], axis=0)
            power = squares(both, second_ref[...])
            psum[r * ROOT + side * HALF : r * ROOT + (side + 1) * HALF, :] = power[:HALF] + on * power[HALF:]
    for r in range(ROWS):
        put(r, jnp.transpose(psum[r * ROOT : (r + 1) * ROOT, :]))
    edge_power = squares(ebuf[...], second_ref[...])
    for side, on in ((0, right_on), (1, left_on)):
        at = side * 2 * ROWS
        mixed = edge_power[at : at + ROWS] + on * edge_power[at + ROWS : at + 2 * ROWS]
        put_edge(side, jnp.where(lane % (2 * per_dev) < per_dev, mixed, jnp.broadcast_to(nyq[side], (ROWS, ROOT))))


def compute_kernel(
    lo_ref, hi_ref, right_ref, left_ref, window_ref, first_ref, second_ref, twist_ref,
    sums_ref, edge_ref, buf, zbuf, ebuf, psum,
):
    me = lax.axis_index("tm")
    count = lax.axis_size("tm")
    right_on = (me < count - 1).astype(jnp.float32)
    left_on = (me > 0).astype(jnp.float32)

    def put(r, value):
        sums_ref[:, r, :] = value

    def put_edge(side, value):
        edge_ref[side] = value

    group_sums(
        lo_ref, hi_ref, right_ref, left_ref, right_on, left_on, HALF // count,
        (window_ref, first_ref, second_ref, twist_ref), (buf, zbuf, ebuf, psum), put, put_edge,
    )


def shifted(block, distance):
    count = lax.axis_size("tm")
    route = [(i - distance, i) for i in range(count) if 0 <= i - distance < count]
    return lax.ppermute(block, "tm", route)


def per_device(strain):
    chan_rows, time_width = strain.shape
    seg_len = ROOT * ROOT
    half_len = seg_len // 2
    assert time_width == seg_len and chan_rows % (2 * ROWS) == 0
    tm_count = lax.axis_size("tm")
    segments = 2 * tm_count - 1
    band = half_len // tm_count
    per_dev = HALF // tm_count
    first_all, second_all, twist, window, energy = tables(tm_count)
    pairs = chan_rows // 2
    groups = pairs // ROWS
    right = shifted(strain[:pairs, :half_len], -1)
    left = shifted(strain[pairs:, half_len:], 1)
    full = lambda shape: pl.BlockSpec(shape, lambda g: (0,) * len(shape))
    sums, edges = pl.pallas_call(
        compute_kernel,
        grid=(groups,),
        in_specs=[
            pl.BlockSpec((ROWS, seg_len), lambda g: (g, 0)),
            pl.BlockSpec((ROWS, seg_len), lambda g: (g + groups, 0)),
            pl.BlockSpec((ROWS, half_len), lambda g: (g, 0)),
            pl.BlockSpec((ROWS, half_len), lambda g: (g, 0)),
            full(window.shape), full(first_all.shape), full(second_all.shape), full(twist.shape),
        ],
        out_specs=[
            pl.BlockSpec((ROOT, ROWS, ROOT), lambda g: (0, g, 0)),
            pl.BlockSpec((2, ROWS, ROOT), lambda g: (0, g, 0)),
        ],
        out_shape=[
            jax.ShapeDtypeStruct((ROOT, pairs, ROOT), jnp.float32),
            jax.ShapeDtypeStruct((2, pairs, ROOT), jnp.float32),
        ],
        scratch_shapes=[
            pltpu.VMEM((ROWS * ROOT, ROOT), jnp.float32),
            pltpu.VMEM((2 * ROWS * HALF, 6 * ROOT), jnp.bfloat16),
            pltpu.VMEM((4 * ROWS, 6 * ROOT), jnp.bfloat16),
            pltpu.VMEM((ROWS * ROOT, ROOT), jnp.float32),
        ],
        name="periodograms",
    )(strain, strain, right, left, window, first_all, second_all, twist)
    mine = lax.psum_scatter(sums, "tm", scatter_dimension=0, tiled=True)
    edges = lax.psum(edges, "tm")
    me = lax.axis_index("tm")
    own_edges = lax.dynamic_slice_in_dim(edges, me * 2 * per_dev, per_dev, axis=2)
    front, back = mine[:per_dev], mine[per_dev:]
    halves = []
    for side in range(2):
        lanes = slice(side * HALF, (side + 1) * HALF)
        middle = jnp.transpose(own_edges[side])[:, :, None]
        mirrored = jnp.flip(back[:, :, lanes][:, :, 1:], axis=2)
        joined = jnp.concatenate([front[:, :, lanes], middle, mirrored], axis=2)
        halves.append(jnp.transpose(joined, (1, 0, 2)).reshape(pairs, band))
    band_total = jnp.concatenate(halves, axis=0)
    bin_index = me * band + jnp.arange(band, dtype=jnp.int32)
    doubling = jnp.where(bin_index == 0, 1.0, 2.0).astype(jnp.float32) / (segments * energy)
    power = band_total * doubling
    nyquist = edges[:, :, per_dev].reshape(chan_rows) / (segments * energy)
    channel_sum = lax.psum(jnp.sum(power, axis=0), "chan")
    mean_power = channel_sum / (chan_rows * lax.axis_size("chan"))
    return (power, nyquist, mean_power)


def solution(mesh):
    in_specs = (P("chan", "tm"),)
    out_specs = (P("chan", "tm"), P("chan"), P("tm"))
    return jax.shard_map(
        per_device, mesh=mesh, in_specs=in_specs, out_specs=out_specs, check_vma=False
    )
```

time: 466 us -> 235 us (0.50); the launches traced: 459 us -> 234 us
  matrix products: 216 us -> 0 us
  waiting for transfers between devices: 63.8 us -> 160 us
  blocking collectives: 85.6 us -> 9.81 us
  other arithmetic: 37.6 us -> 3.14 us
  Pallas kernels: 0 us -> 32.5 us
  local copies, waits for them, and re-layouts: 40.1 us -> 9.21 us
  starting transfers between devices: 1.32 us -> 6.04 us
    dot_general x12 -> x0, matrix products: 216 us -> none  [the longest x2 49.2 us: periodogram(): jnp.einsum('ka,rab->rkb', sin_short, folded, precision=highest_mode)]
    psum x0 -> x1, waiting for transfers between devices: none -> 85.4 us  [per_device(): edges = lax.psum(edges, 'tm')]
    psum x1 -> x0, blocking collectives: 75.8 us -> none  [per_device(): edges_total = lax.psum(nyquist_part, 'tm')]
    unnamed x17 -> x4, local copies, waits for them, and re-layouts: 33.8 us -> 0.01 us
    reduce_sum x3 -> x0, other arithmetic: 33.5 us -> none  [the longest x1 22.8 us: periodogram(): edge_term = jnp.sum(folded * parity, axis=(1, 2))]
    pallas_call x0 -> x1, Pallas kernels: none -> 32.5 us  [per_device(): pl.pallas_call(compute_kernel, grid=(groups,), in_specs=[pl.BlockSpec((RO...]
    reduce_scatter x1, waiting for transfers between devices: 53.7 us -> 69.7 us  [per_device(): mine = lax.psum_scatter(sums, 'tm', scatter_dimension=0, tiled=True)]
    ppermute x1 -> x2, waiting for transfers between devices: 10.1 us -> 3.77 us  [shifted(): return lax.ppermute(block, 'tm', route)]
  transfers between devices with their start and end apart: 2 -> 4, of which waited for: 2 -> 4; matrix products, arithmetic and copies ran while one was open for 1% -> 2% of each run, Pallas kernels for 0% -> 0%
where the time goes in v1:
time: 235 us; the launch traced here: 234 us
  waiting for transfers between devices  160 us (68%)
  Pallas kernels  32.5 us (14%)
  between operations  14.1 us (6%)
  blocking collectives  9.81 us (4%)
  local copies, waits for them, and re-layouts  9.21 us (4%)
  starting transfers between devices  6.04 us (3%)
  other arithmetic  3.14 us (1%)
    psum x1, waiting for transfers between devices, per_device(): edges = lax.psum(edges, 'tm')  85.4 us
    reduce_scatter x1, waiting for transfers between devices, per_device(): mine = lax.psum_scatter(sums, 'tm', scatter_dimension=0, tiled=True)  69.7 us
    pallas_call x1, Pallas kernels, per_device(): pl.pallas_call(compute_kernel, grid=(groups,), in_specs=[pl.BlockSpec((RO...  32.5 us
    psum x1, blocking collectives, per_device(): channel_sum = lax.psum(jnp.sum(power, axis=0), 'chan')  9.81 us
    ppermute x2, starting transfers between devices, shifted(): return lax.ppermute(block, 'tm', route)  5.96 us
  transfers between devices with their start and end apart: 4, of which 4 were waited for; matrix products, arithmetic and copies ran while one was open for 2% of the time, Pallas kernels for 0%

profile of v1, /device:TPU:0, one launch (start us, length us, event | category | flops | bytes accessed | tf_op | source)
XLA Modules:
  0.0 234.4 jit_solution(1440886341234220441)
XLA Ops:
  7.2 0.0 all-reduce.2.cloned.1.call-start
  7.2 3.3 %fusion.2 = (f32[96,8192]{1,0:T(8,128)S(1)}, f32[96,8192]{1,0:T(8,128)S(1)}) fusion(f32[192,16384]{1,0:T(8,128)} %hi_ref.1), kind=kLoop, calls=%fused_computation.13 | loop fusion | bytes 12582912 | tf_op jit(solution)/shard_map/slice | solution.py:183
  10.5 1.3 collective-permute-start
  11.8 4.7 %collective-permute-start.1 = (f32[96,8192]{1,0:T(8,128)S(1)}, f32[96,8192]{1,0:T(8,128)}, u32[]{:S(2)}, u32[]{:S(2)}) collective-permute-start(f32[96,8192]{1,0:T(8,128)S(1)} %get-tuple-element.9), channel_id=1, source_target_pairs={{0,1},{1,2},{2,3},{3,4},{4,5},{5,6},{6,7},{8,9},{9,10},{10,11},{11... | collective-permute-start | bytes 9437192 | tf_op jit(solution)/shard_map/ppermute | solution.py:167
  16.4 1.6 collective-permute-done.right_ref
  18.0 0.0 copy-start
  18.0 2.2 collective-permute-done.1.left_ref
  20.2 0.0 copy-done
  20.2 32.5 %periodograms.1 = (f32[128,96,128]{2,1,0:T(8,128)}, f32[2,96,128]{2,1,0:T(8,128)}) custom-call(f32[192,16384]{1,0:T(8,128)} %hi_ref.1, f32[192,16384]{1,0:T(8,128)} %hi_ref.1, f32[96,8192]{1,0:T(8,128)} %copy-done, f32[96,8192]{1,0:T(8,128)} %collective-permute-done.1.left_ref, f32[128,128]{1,0:T(8,128)} %constant.37.clone.window_ref, ...), custom_call_target="tpu_custom_call" | custom-call | tf_op jit(solution)/shard_map/periodograms/pallas_call | solution.py:185
  52.8 0.0 all-reduce.2.cloned.1.call-update
  52.8 0.0 reduce-scatter.2.cloned.1.call-start
  52.8 0.7 reduce-scatter.2.cloned.1.call-update
  53.5 85.4 %all-reduce.2.cloned.1.call-done = f32[2,96,128]{2,1,0:T(8,128)} async-done(((f32[2,96,128]{2,1,0:T(8,128)}), f32[2,96,128]{2,1,0:T(8,128)}) %all-reduce.2.cloned.1.call-update) | async-done | bytes 98320 | tf_op jit(solution)/shard_map/psum | solution.py:212
  139.0 0.9 dynamic-slice_bitcast_fusion.1
  139.9 0.7 copy.10
  140.6 0.7 copy.12
  141.2 1.1 fusion
  142.3 0.7 div.24
  142.9 69.7 %reduce-scatter.2.cloned.1.call-done = f32[16,96,128]{2,1,0:T(8,128)} async-done(((f32[128,96,128]{2,1,0:T(8,128)}), f32[16,96,128]{2,1,0:T(8,128)}) %reduce-scatter.2.cloned.1.call-update) | async-done | bytes 786448 | tf_op jit(solution)/shard_map/reduce_scatter | solution.py:211
  212.6 0.0 copy-start.1
  212.6 1.5 fusion.4
  214.1 0.7 rev.7
  214.8 0.7 rev.8
  215.5 0.0 copy-done.1
  215.5 0.2 fusion.3
  215.7 0.5 maximum_bitcast_fusion
  216.2 1.0 fusion.1
  217.2 9.8 %psum.15 = f32[1024]{0:T(1024)S(1)} all-reduce(f32[1024]{0:T(1024)S(1)} %get-tuple-element.7), channel_id=1, replica_groups=mesh['chan'=4,'tm'=8] {'chan'}, use_global_device_ids=true, to_apply=%region_3.4 | all-reduce | flops 1024 | bytes 8192 | tf_op jit(solution)/shard_map/psum | solution.py:228
  227.0 0.6 broadcast_multiply_fusion
  (3 shorter events, 0.1 us)
Async XLA Ops:
  7.2 131.8 %all-reduce.2.cloned.1.call-start = ((), (), s32[]{:S(2)}) async-start(), calls=%async_computation.2 | async-start | bytes 196608 | tf_op jit(solution)/shard_map/psum | solution.py:212
  10.5 7.6 %collective-permute-start = (f32[96,8192]{1,0:T(8,128)S(1)}, f32[96,8192]{1,0:T(8,128)S(1)}, u32[]{:S(2)}, u32[]{:S(2)}) collective-permute-start(f32[96,8192]{1,0:T(8,128)S(1)} %get-tuple-element.10), channel_id=1, source_target_pairs={{1,0},{2,1},{3,2},{4,3},{5,4},{6,5},{7,6},{9,8},{10,9},{11,10},{12... | collective-permute-start | bytes 9437192 | tf_op jit(solution)/shard_map/ppermute | solution.py:167
  11.8 8.4 %collective-permute-start.1 = (f32[96,8192]{1,0:T(8,128)S(1)}, f32[96,8192]{1,0:T(8,128)}, u32[]{:S(2)}, u32[]{:S(2)}) collective-permute-start(f32[96,8192]{1,0:T(8,128)S(1)} %get-tuple-element.9), channel_id=1, source_target_pairs={{0,1},{1,2},{2,3},{3,4},{4,5},{5,6},{6,7},{8,9},{9,10},{10,11},{11... | collective-permute-start | bytes 9437192 | tf_op jit(solution)/shard_map/ppermute | solution.py:167
  18.0 2.2 copy-start
  52.8 159.9 %reduce-scatter.2.cloned.1.call-start = ((), (), s32[]{:S(2)}) async-start(), calls=%async_computation.1 | async-start | bytes 7077888 | tf_op jit(solution)/shard_map/reduce_scatter | solution.py:211
  212.6 2.8 %copy-start.1 = (f32[16,96,128]{2,1,0:T(8,128)S(1)}, f32[16,96,128]{2,1,0:T(8,128)}, u32[]{:S(2)}) copy-start(f32[16,96,128]{2,1,0:T(8,128)} %reduce-scatter.2.cloned.1.call-done) | copy-start | bytes 2359300
Sparse Core Ops, SparseCore 0:
  52.9 86.0 all-reduce.1
  141.3 71.3 reduce-scatter.1

commit v2 on v1

--- a/solution.py
+++ b/solution.py
@@ -140,31 +140,182 @@
         put_edge(side, jnp.where(lane % (2 * per_dev) < per_dev, mixed, jnp.broadcast_to(nyq[side], (ROWS, ROOT))))
 
 
-def compute_kernel(
-    lo_ref, hi_ref, right_ref, left_ref, window_ref, first_ref, second_ref, twist_ref,
-    sums_ref, edge_ref, buf, zbuf, ebuf, psum,
+def welch_kernel(
+    pieces, strain_ref, window_ref, first_ref, second_ref, twist_ref, mine_ref, edge_out_ref,
+    data, right_half, left_half, sums, edge_rows, edge_sums, from_left, from_right, edge_left, edge_right,
+    buf, zbuf, ebuf, psum,
+    load_sem, halo_send, halo_recv, line_send, line_recv, edge_send, edge_recv,
 ):
     me = lax.axis_index("tm")
     count = lax.axis_size("tm")
-    right_on = (me < count - 1).astype(jnp.float32)
-    left_on = (me > 0).astype(jnp.float32)
-
-    def put(r, value):
-        sums_ref[:, r, :] = value
-
-    def put_edge(side, value):
-        edge_ref[side] = value
-
-    group_sums(
-        lo_ref, hi_ref, right_ref, left_ref, right_on, left_on, HALF // count,
-        (window_ref, first_ref, second_ref, twist_ref), (buf, zbuf, ebuf, psum), put, put_edge,
-    )
-
-
-def shifted(block, distance):
-    count = lax.axis_size("tm")
-    route = [(i - distance, i) for i in range(count) if 0 <= i - distance < count]
-    return lax.ppermute(block, "tm", route)
+    per_dev = HALF // count
+    rows = 2 * per_dev
+    half_len = ROOT * HALF
+    pairs = sums.shape[1]
+    groups = pairs // ROWS
+    width = pairs // pieces
+    has_left, has_right = me > 0, me < count - 1
+    right_on, left_on = has_right.astype(jnp.float32), has_left.astype(jnp.float32)
+
+    def block(g, side):
+        return pl.ds(pl.multiple_of(side * pairs + g * ROWS, ROWS), ROWS)
+
+    def load(g, side):
+        return pltpu.make_async_copy(
+            strain_ref.at[block(g, side)], data.at[block(g, side)], load_sem.at[side, g]
+        )
+
+    def halo(g, side):
+        source = strain_ref.at[block(g, side), pl.ds(side * half_len, half_len)]
+        target = (right_half, left_half)[side]
+        return pltpu.make_async_remote_copy(
+            src_ref=source, dst_ref=target.at[block(g, 0)],
+            send_sem=halo_send.at[side, g], recv_sem=halo_recv.at[side, g],
+            device_id={"tm": me + (1 if side else -1)}, device_id_type=pl.DeviceIdType.MESH,
+        )
+
+    @pl.loop(0, groups)
+    def _(g):
+        load(g, 0).start()
+        load(g, 1).start()
+
+    barrier = pltpu.get_barrier_semaphore()
+    for exists, step in ((has_left, -1), (has_right, 1)):
+        @pl.when(exists)
+        def _():
+            pl.semaphore_signal(
+                barrier, inc=1, device_id={"tm": me + step}, device_id_type=pl.DeviceIdType.MESH
+            )
+    pl.semaphore_wait(barrier, has_left.astype(jnp.int32) + has_right.astype(jnp.int32))
+
+    @pl.loop(0, groups)
+    def _(g):
+        for side, exists in ((0, has_left), (1, has_right)):
+            @pl.when(exists)
+            def _():
+                halo(g, side).start()
+
+    edge_rows[...] = jnp.zeros_like(edge_rows)
+    for side, exists, ref in ((0, has_right, right_half), (1, has_left, left_half)):
+        @pl.when(jnp.logical_not(exists))
+        def _():
+            ref[...] = jnp.zeros_like(ref)
+
+    @pl.loop(0, groups)
+    def _(g):
+        load(g, 0).wait()
+        load(g, 1).wait()
+        for side, exists in ((0, has_right), (1, has_left)):
+            @pl.when(exists)
+            def _():
+                halo(g, side).wait_recv()
+
+        def put(r, value):
+            sums[:, g * ROWS + r, :] = value
+
+        def put_edge(side, value):
+            edge_rows[block(g, side), :] = value
+
+        group_sums(
+            data.at[block(g, 0)], data.at[block(g, 1)], right_half.at[block(g, 0)], left_half.at[block(g, 0)],
+            right_on, left_on, per_dev,
+            (window_ref, first_ref, second_ref, twist_ref), (buf, zbuf, ebuf, psum), put, put_edge,
+        )
+
+    spread = edge_sums.shape[1]
+    for s in range(spread):
+        edge_sums[:, s, :] = jnp.transpose(edge_rows[s * ROOT : (s + 1) * ROOT, :])
+
+    def chunk_of(m, side):
+        far = m // pieces
+        return far if side else count - 1 - far
+
+    def sum_part(m, side):
+        q = lax.rem(m, pieces)
+        return sums.at[pl.ds(chunk_of(m, side) * rows, rows), pl.ds(pl.multiple_of(q * width, ROWS), width)]
+
+    def edge_part(m, side):
+        return edge_sums.at[pl.ds(chunk_of(m, side) * rows, rows)]
+
+    def line(m, side):
+        target = (from_left, from_right)[side]
+        return pltpu.make_async_remote_copy(
+            src_ref=sum_part(m, side), dst_ref=target.at[m],
+            send_sem=line_send.at[side, m], recv_sem=line_recv.at[side, m],
+            device_id={"tm": me + (-1 if side else 1)}, device_id_type=pl.DeviceIdType.MESH,
+        )
+
+    def edge_line(m, side):
+        target = (edge_left, edge_right)[side]
+        far = m // pieces
+        return pltpu.make_async_remote_copy(
+            src_ref=edge_part(m, side), dst_ref=target.at[far],
+            send_sem=edge_send.at[side, far], recv_sem=edge_recv.at[side, far],
+            device_id={"tm": me + (-1 if side else 1)}, device_id_type=pl.DeviceIdType.MESH,
+        )
+
+    def take(m, side):
+        line(m, side).wait_recv()
+        part = sum_part(m, side)
+        part[...] = part[...] + (from_left, from_right)[side][m]
+
+        @pl.when(lax.rem(m, pieces) == 0)
+        def _():
+            edge_line(m, side).wait_recv()
+            edge = edge_part(m, side)
+            edge[...] = edge[...] + (edge_left, edge_right)[side][m // pieces]
+
+    messages = (count - 1) * pieces
+
+    @pl.loop(0, messages + count - 1)
+    def _(t):
+        for side in range(2):
+            place = count - 1 - me if side else me
+            m = t - place
+
+            @pl.when(jnp.logical_and(m >= 0, m < (count - 1 - place) * pieces))
+            def _():
+                @pl.when(place > 0)
+                def _():
+                    take(m, side)
+
+                line(m, side).start()
+
+                @pl.when(lax.rem(m, pieces) == 0)
+                def _():
+                    edge_line(m, side).start()
+
+    for side in range(2):
+        place = count - 1 - me if side else me
+
+        @pl.when(place > 0)
+        def _():
+            @pl.loop(0, pieces)
+            def _(q):
+                take((count - 1 - place) * pieces + q, side)
+
+    mine_ref[...] = sums[pl.ds(me * rows, rows)]
+    edge_out_ref[...] = edge_sums[pl.ds(me * rows, rows)]
+
+    @pl.loop(0, groups)
+    def _(g):
+        for side, exists in ((0, has_left), (1, has_right)):
+            @pl.when(exists)
+            def _():
+                halo(g, side).wait_send()
+
+    @pl.loop(0, messages)
+    def _(m):
+        for side in range(2):
+            place = count - 1 - me if side else me
+
+            @pl.when(m < (count - 1 - place) * pieces)
+            def _():
+                line(m, side).wait_send()
+
+                @pl.when(lax.rem(m, pieces) == 0)
+                def _():
+                    edge_line(m, side).wait_send()
 
 
 def per_device(strain):
@@ -176,55 +327,66 @@
     segments = 2 * tm_count - 1
     band = half_len // tm_count
     per_dev = HALF // tm_count
+    rows = 2 * per_dev
     first_all, second_all, twist, window, energy = tables(tm_count)
     pairs = chan_rows // 2
     groups = pairs // ROWS
-    right = shifted(strain[:pairs, :half_len], -1)
-    left = shifted(strain[pairs:, half_len:], 1)
-    full = lambda shape: pl.BlockSpec(shape, lambda g: (0,) * len(shape))
-    sums, edges = pl.pallas_call(
-        compute_kernel,
-        grid=(groups,),
-        in_specs=[
-            pl.BlockSpec((ROWS, seg_len), lambda g: (g, 0)),
-            pl.BlockSpec((ROWS, seg_len), lambda g: (g + groups, 0)),
-            pl.BlockSpec((ROWS, half_len), lambda g: (g, 0)),
-            pl.BlockSpec((ROWS, half_len), lambda g: (g, 0)),
-            full(window.shape), full(first_all.shape), full(second_all.shape), full(twist.shape),
-        ],
-        out_specs=[
-            pl.BlockSpec((ROOT, ROWS, ROOT), lambda g: (0, g, 0)),
-            pl.BlockSpec((2, ROWS, ROOT), lambda g: (0, g, 0)),
-        ],
+    pieces = 4 if groups % 4 == 0 else 1
+    spread = -(-chan_rows // ROOT)
+    messages = (tm_count - 1) * pieces
+    vmem = pl.BlockSpec(memory_space=pltpu.VMEM)
+    f32 = jnp.float32
+    mine, own_edges = pl.pallas_call(
+        functools.partial(welch_kernel, pieces),
+        in_specs=[pl.BlockSpec(memory_space=pl.ANY)] + [vmem] * 4,
+        out_specs=[vmem, vmem],
         out_shape=[
-            jax.ShapeDtypeStruct((ROOT, pairs, ROOT), jnp.float32),
-            jax.ShapeDtypeStruct((2, pairs, ROOT), jnp.float32),
+            jax.ShapeDtypeStruct((rows, pairs, ROOT), f32),
+            jax.ShapeDtypeStruct((rows, spread, ROOT), f32),
         ],
         scratch_shapes=[
-            pltpu.VMEM((ROWS * ROOT, ROOT), jnp.float32),
+            pltpu.VMEM((chan_rows, seg_len), f32),
+            pltpu.VMEM((pairs, half_len), f32),
+            pltpu.VMEM((pairs, half_len), f32),
+            pltpu.VMEM((ROOT, pairs, ROOT), f32),
+            pltpu.VMEM((spread * ROOT, ROOT), f32),
+            pltpu.VMEM((ROOT, spread, ROOT), f32),
+            pltpu.VMEM((messages, rows, pairs // pieces, ROOT), f32),
+            pltpu.VMEM((messages, rows, pairs // pieces, ROOT), f32),
+            pltpu.VMEM((tm_count - 1, rows, spread, ROOT), f32),
+            pltpu.VMEM((tm_count - 1, rows, spread, ROOT), f32),
+            pltpu.VMEM((ROWS * ROOT, ROOT), f32),
             pltpu.VMEM((2 * ROWS * HALF, 6 * ROOT), jnp.bfloat16),
             pltpu.VMEM((4 * ROWS, 6 * ROOT), jnp.bfloat16),
-            pltpu.VMEM((ROWS * ROOT, ROOT), jnp.float32),
+            pltpu.VMEM((ROWS * ROOT, ROOT), f32),
+            pltpu.SemaphoreType.DMA((2, groups)),
+            pltpu.SemaphoreType.DMA((2, groups)),
+            pltpu.SemaphoreType.DMA((2, groups)),
+            pltpu.SemaphoreType.DMA((2, messages)),
+            pltpu.SemaphoreType.DMA((2, messages)),
+            pltpu.SemaphoreType.DMA((2, tm_count - 1)),
+            pltpu.SemaphoreType.DMA((2, tm_count - 1)),
         ],
-        name="periodograms",
-    )(strain, strain, right, left, window, first_all, second_all, twist)
-    mine = lax.psum_scatter(sums, "tm", scatter_dimension=0, tiled=True)
-    edges = lax.psum(edges, "tm")
+        compiler_params=pltpu.CompilerParams(
+            collective_id=0, has_side_effects=True, vmem_limit_bytes=60 * 2**20
+        ),
+        name="welch",
+    )(strain, window, first_all, second_all, twist)
     me = lax.axis_index("tm")
-    own_edges = lax.dynamic_slice_in_dim(edges, me * 2 * per_dev, per_dev, axis=2)
     front, back = mine[:per_dev], mine[per_dev:]
+    middle = own_edges[:per_dev].reshape(per_dev, -1)[:, :chan_rows]
     halves = []
     for side in range(2):
         lanes = slice(side * HALF, (side + 1) * HALF)
-        middle = jnp.transpose(own_edges[side])[:, :, None]
         mirrored = jnp.flip(back[:, :, lanes][:, :, 1:], axis=2)
-        joined = jnp.concatenate([front[:, :, lanes], middle, mirrored], axis=2)
+        centre = middle[:, side * pairs : (side + 1) * pairs, None]
+        joined = jnp.concatenate([front[:, :, lanes], centre, mirrored], axis=2)
         halves.append(jnp.transpose(joined, (1, 0, 2)).reshape(pairs, band))
     band_total = jnp.concatenate(halves, axis=0)
     bin_index = me * band + jnp.arange(band, dtype=jnp.int32)
     doubling = jnp.where(bin_index == 0, 1.0, 2.0).astype(jnp.float32) / (segments * energy)
     power = band_total * doubling
-    nyquist = edges[:, :, per_dev].reshape(chan_rows) / (segments * energy)
+    nyquist = own_edges[per_dev].reshape(-1)[:chan_rows] / (segments * energy)
     channel_sum = lax.psum(jnp.sum(power, axis=0), "chan")
     mean_power = channel_sum / (chan_rows * lax.axis_size("chan"))
     return (power, nyquist, mean_power)

time: 235 us -> 124 us (0.53)
  the two profiles are of different devices: /device:TPU:0 before, /device:TPU:8 now
where the time goes in v2:
time: 124 us
  Pallas kernels  105 us (85%)
  blocking collectives  9.88 us (8%)
  local copies, waits for them, and re-layouts  5.92 us (5%)
  other arithmetic  2.64 us (2%)
    pallas_call x1, Pallas kernels, per_device(): pl.pallas_call(functools.partial(welch_kernel, pieces), in_specs=[pl.Bloc...  105 us
    psum x1, blocking collectives, per_device(): channel_sum = lax.psum(jnp.sum(power, axis=0), 'chan')  9.88 us

profile of v2, /device:TPU:8, one launch (start us, length us, event | category | flops | bytes accessed | tf_op | source)
XLA Modules:
  0.0 123.7 jit_solution(16612284115486880905)
XLA Ops:
  0.6 104.6 %welch.1 = (f32[16,96,128]{2,1,0:T(8,128)}, f32[16,2,128]{2,1,0:T(2,128)}) custom-call(f32[192,16384]{1,0:T(8,128)} %strain_ref.1, f32[128,128]{1,0:T(8,128)} %constant.30.clone.window_ref, bf16[256,256]{1,0:T(8,128)(2,1)} %constant.31.clone.first_ref, bf16[768,256]{1,0:T(8,128)(2,1)} %constant.32.clone.second_ref, f32[72,256]{1,0:T(8,128)} %constant.33.clone.twist_ref), custom_call_target="tpu_custom_call" | custom-call | tf_op jit(solution)/shard_map/welch/pallas_call | solution.py:339
  105.2 0.7 slice_bitcast_fusion.3
  105.9 0.7 slice_bitcast_fusion
  106.6 0.6 slice_multiply_fusion
  107.2 0.1 slice_bitcast_fusion.2
  107.3 0.2 copy.12
  107.4 0.2 copy.14
  107.6 1.4 %fusion.2 = (f32[8,96,63]{2,1,0:T(8,128)S(1)}, f32[8,96,63]{2,1,0:T(8,128)S(1)}) fusion(f32[16,96,128]{2,1,0:T(8,128)} %get-tuple-element.5), kind=kLoop, calls=%fused_computation.16 | loop fusion | bytes 774144 | tf_op jit(solution)/shard_map/slice | solution.py:381
  109.0 0.7 rev.7
  109.7 1.3 %fusion.1 = (f32[8,96,64]{2,1,0:T(8,128)S(1)}, f32[8,96,64]{2,1,0:T(8,128)S(1)}) fusion(f32[16,96,128]{2,1,0:T(8,128)} %get-tuple-element.5), kind=kLoop, calls=%fused_computation.15 | loop fusion | bytes 786432 | tf_op jit(solution)/shard_map/slice | solution.py:383
  111.0 0.7 rev.8
  111.7 0.5 maximum_bitcast_fusion
  112.3 1.0 fusion
  113.2 9.9 %psum.7 = f32[1024]{0:T(1024)S(1)} all-reduce(f32[1024]{0:T(1024)S(1)} %get-tuple-element.7), channel_id=1, replica_groups=mesh['chan'=4,'tm'=8] {'chan'}, use_global_device_ids=true, to_apply=%region_1.2 | all-reduce | flops 1024 | bytes 8192 | tf_op jit(solution)/shard_map/psum | solution.py:390
  123.1 0.6 broadcast_multiply_fusion
  (4 shorter events, 0.1 us)

commit v3 on v2

--- a/solution.py
+++ b/solution.py
@@ -44,10 +44,16 @@
     second_all = np.concatenate([second_hi, second_hi, second_lo], axis=0)
     long = 2.0 * np.pi * np.outer(np.arange(HALF + ROWS), pos) / (ROOT * ROOT)
     twist = np.concatenate([np.cos(long), np.sin(long)], axis=1).astype(np.float32)
+    mirror = np.zeros((2 * ROOT, 2 * ROOT), np.float32)
+    for side in range(2):
+        for k in range(HALF):
+            mirror[side * HALF + k, side * ROOT + k] = 1.0
+            if k > 0:
+                mirror[ROOT + side * HALF + k, side * ROOT + ROOT - k] = 1.0
     seg_len = ROOT * ROOT
     window = 0.5 - 0.5 * np.cos(2.0 * np.pi * np.arange(seg_len) / seg_len)
     energy = float(np.sum(window * window))
-    return first_all, second_all, twist, window.reshape(ROOT, ROOT).astype(np.float32), energy
+    return first_all, second_all, twist, window.reshape(ROOT, ROOT).astype(np.float32), mirror, energy
 
 
 def split(value):
@@ -141,11 +147,13 @@
 
 
 def welch_kernel(
-    pieces, strain_ref, window_ref, first_ref, second_ref, twist_ref, mine_ref, edge_out_ref,
+    pieces, scale, strain_ref, window_ref, first_ref, second_ref, twist_ref, mirror_ref,
+    power_ref, nyquist_ref, mean_ref,
     data, right_half, left_half, sums, edge_rows, edge_sums, from_left, from_right, edge_left, edge_right,
-    buf, zbuf, ebuf, psum,
-    load_sem, halo_send, halo_recv, line_send, line_recv, edge_send, edge_recv,
+    buf, zbuf, ebuf, psum, channel_sums, channel_from,
+    load_sem, halo_send, halo_recv, line_send, line_recv, edge_send, edge_recv, chan_send, chan_recv,
 ):
+    chan, chan_count = lax.axis_index("chan"), lax.axis_size("chan")
     me = lax.axis_index("tm")
     count = lax.axis_size("tm")
     per_dev = HALF // count
@@ -186,7 +194,14 @@
             pl.semaphore_signal(
                 barrier, inc=1, device_id={"tm": me + step}, device_id_type=pl.DeviceIdType.MESH
             )
-    pl.semaphore_wait(barrier, has_left.astype(jnp.int32) + has_right.astype(jnp.int32))
+    for k in range(1, chan_count):
+        pl.semaphore_signal(
+            barrier, inc=1, device_id={"chan": lax.rem(chan + k, chan_count)},
+            device_id_type=pl.DeviceIdType.MESH,
+        )
+    pl.semaphore_wait(
+        barrier, has_left.astype(jnp.int32) + has_right.astype(jnp.int32) + (chan_count - 1)
+    )
 
     @pl.loop(0, groups)
     def _(g):
@@ -294,8 +309,38 @@
             def _(q):
                 take((count - 1 - place) * pieces + q, side)
 
-    mine_ref[...] = sums[pl.ds(me * rows, rows)]
-    edge_out_ref[...] = edge_sums[pl.ds(me * rows, rows)]
+    nyquist_ref[...] = edge_sums[me * rows + per_dev] * scale
+    for s in range(spread):
+        strip = jnp.concatenate(
+            [edge_sums[me * rows + j, s : s + 1, :] for j in range(per_dev)]
+            + [jnp.zeros((ROOT - per_dev, ROOT), jnp.float32)],
+            axis=0,
+        )
+        edge_rows[s * ROOT : (s + 1) * ROOT, :] = jnp.transpose(strip)
+    lanes = lax.broadcasted_iota(jnp.int32, (1, ROOT), 1)
+    for j in range(per_dev):
+        both = jnp.concatenate([sums[me * rows + j], sums[me * rows + per_dev + j]], axis=1)
+        placed = jnp.dot(
+            both, mirror_ref[...], precision=lax.Precision.HIGHEST, preferred_element_type=jnp.float32
+        )
+        factor = jnp.where(jnp.logical_and(lanes == 0, me + j == 0), scale, 2.0 * scale)
+        column = jnp.zeros((1, ROOT), jnp.float32)
+        for side in range(2):
+            middle = edge_rows[side * pairs : (side + 1) * pairs, j : j + 1]
+            value = jnp.where(lanes == HALF, middle, placed[:, side * ROOT : (side + 1) * ROOT]) * factor
+            power_ref[side * pairs : (side + 1) * pairs, j * ROOT : (j + 1) * ROOT] = value
+            column = column + jnp.sum(value, axis=0, keepdims=True)
+        channel_sums[j : j + 1, :] = column
+
+    def chan_copy(k):
+        return pltpu.make_async_remote_copy(
+            src_ref=channel_sums, dst_ref=channel_from.at[k],
+            send_sem=chan_send.at[k], recv_sem=chan_recv.at[k],
+            device_id={"chan": lax.rem(chan + k, chan_count)}, device_id_type=pl.DeviceIdType.MESH,
+        )
+
+    for k in range(1, chan_count):
+        chan_copy(k).start()
 
     @pl.loop(0, groups)
     def _(g):
@@ -316,6 +361,14 @@
                 @pl.when(lax.rem(m, pieces) == 0)
                 def _():
                     edge_line(m, side).wait_send()
+
+    channel_from[0] = channel_sums[...]
+    for k in range(1, chan_count):
+        chan_copy(k).wait()
+    total = jnp.zeros_like(channel_sums)
+    for source in range(chan_count):
+        total = total + channel_from[lax.rem(chan - source + chan_count, chan_count)]
+    mean_ref[...] = total * (1.0 / (2 * pairs * chan_count))
 
 
 def per_device(strain):
@@ -328,7 +381,7 @@
     band = half_len // tm_count
     per_dev = HALF // tm_count
     rows = 2 * per_dev
-    first_all, second_all, twist, window, energy = tables(tm_count)
+    first_all, second_all, twist, window, mirror, energy = tables(tm_count)
     pairs = chan_rows // 2
     groups = pairs // ROWS
     pieces = 4 if groups % 4 == 0 else 1
@@ -336,13 +389,14 @@
     messages = (tm_count - 1) * pieces
     vmem = pl.BlockSpec(memory_space=pltpu.VMEM)
     f32 = jnp.float32
-    mine, own_edges = pl.pallas_call(
-        functools.partial(welch_kernel, pieces),
-        in_specs=[pl.BlockSpec(memory_space=pl.ANY)] + [vmem] * 4,
-        out_specs=[vmem, vmem],
+    power, nyquist, mean_power = pl.pallas_call(
+        functools.partial(welch_kernel, pieces, 1.0 / (segments * energy)),
+        in_specs=[pl.BlockSpec(memory_space=pl.ANY)] + [vmem] * 5,
+        out_specs=[vmem] * 3,
         out_shape=[
-            jax.ShapeDtypeStruct((rows, pairs, ROOT), f32),
-            jax.ShapeDtypeStruct((rows, spread, ROOT), f32),
+            jax.ShapeDtypeStruct((chan_rows, band), f32),
+            jax.ShapeDtypeStruct((spread, ROOT), f32),
+            jax.ShapeDtypeStruct((per_dev, ROOT), f32),
         ],
         scratch_shapes=[
             pltpu.VMEM((chan_rows, seg_len), f32),
@@ -359,6 +413,8 @@
             pltpu.VMEM((2 * ROWS * HALF, 6 * ROOT), jnp.bfloat16),
             pltpu.VMEM((4 * ROWS, 6 * ROOT), jnp.bfloat16),
             pltpu.VMEM((ROWS * ROOT, ROOT), f32),
+            pltpu.VMEM((per_dev, ROOT), f32),
+            pltpu.VMEM((lax.axis_size("chan"), per_dev, ROOT), f32),
             pltpu.SemaphoreType.DMA((2, groups)),
             pltpu.SemaphoreType.DMA((2, groups)),
             pltpu.SemaphoreType.DMA((2, groups)),
@@ -366,30 +422,15 @@
             pltpu.SemaphoreType.DMA((2, messages)),
             pltpu.SemaphoreType.DMA((2, tm_count - 1)),
             pltpu.SemaphoreType.DMA((2, tm_count - 1)),
+            pltpu.SemaphoreType.DMA((lax.axis_size("chan"),)),
+            pltpu.SemaphoreType.DMA((lax.axis_size("chan"),)),
         ],
         compiler_params=pltpu.CompilerParams(
             collective_id=0, has_side_effects=True, vmem_limit_bytes=60 * 2**20
         ),
         name="welch",
-    )(strain, window, first_all, second_all, twist)
-    me = lax.axis_index("tm")
-    front, back = mine[:per_dev], mine[per_dev:]
-    middle = own_edges[:per_dev].reshape(per_dev, -1)[:, :chan_rows]
-    halves = []
-    for side in range(2):
-        lanes = slice(side * HALF, (side + 1) * HALF)
-        mirrored = jnp.flip(back[:, :, lanes][:, :, 1:], axis=2)
-        centre = middle[:, side * pairs : (side + 1) * pairs, None]
-        joined = jnp.concatenate([front[:, :, lanes], centre, mirrored], axis=2)
-        halves.append(jnp.transpose(joined, (1, 0, 2)).reshape(pairs, band))
-    band_total = jnp.concatenate(halves, axis=0)
-    bin_index = me * band + jnp.arange(band, dtype=jnp.int32)
-    doubling = jnp.where(bin_index == 0, 1.0, 2.0).astype(jnp.float32) / (segments * energy)
-    power = band_total * doubling
-    nyquist = own_edges[per_dev].reshape(-1)[:chan_rows] / (segments * energy)
-    channel_sum = lax.psum(jnp.sum(power, axis=0), "chan")
-    mean_power = channel_sum / (chan_rows * lax.axis_size("chan"))
-    return (power, nyquist, mean_power)
+    )(strain, window, first_all, second_all, twist, mirror)
+    return (power, nyquist.reshape(-1)[:chan_rows], mean_power.reshape(-1))
 
 
 def solution(mesh):

time: 124 us -> 115 us (0.927)
  blocking collectives: 9.88 us -> 0 us
  Pallas kernels: 105 us -> 109 us
  other arithmetic: 2.64 us -> 0 us
  local copies, waits for them, and re-layouts: 5.92 us -> 4.57 us
    psum x1 -> x0, blocking collectives: 9.88 us -> none  [per_device(): channel_sum = lax.psum(jnp.sum(power, axis=0), 'chan')]
    pallas_call x1, Pallas kernels: 105 us -> 109 us  [per_device(): pl.pallas_call(functools.partial(welch_kernel, pieces, 1.0 / (segments *...]
    unnamed x2 -> x3, local copies, waits for them, and re-layouts: 0.7 us -> 4.57 us
    slice x2 -> x0, local copies, waits for them, and re-layouts: 2.68 us -> none  [the longest x1 1.39 us: per_device(): mirrored = jnp.flip(back[:, :, lanes][:, :, 1:], axis=2)]
    rev x2 -> x0, local copies, waits for them, and re-layouts: 1.36 us -> none  [per_device(): mirrored = jnp.flip(back[:, :, lanes][:, :, 1:], axis=2)]
where the time goes in v3:
time: 115 us
  Pallas kernels  109 us (95%)
  local copies, waits for them, and re-layouts  4.57 us (4%)
    pallas_call x1, Pallas kernels, per_device(): pl.pallas_call(functools.partial(welch_kernel, pieces, 1.0 / (segments *...  109 us
    unnamed x3, local copies, waits for them, and re-layouts  4.57 us

profile of v3, /device:TPU:8, one launch (start us, length us, event | category | flops | bytes accessed | tf_op | source)
XLA Modules:
  0.0 114.6 jit_solution(1947769160991910729)
XLA Ops:
  0.6 109.3 %welch.1 = (f32[192,1024]{1,0:T(8,128)}, f32[2,128]{1,0:T(2,128)}, f32[8,128]{1,0:T(8,128)}) custom-call(f32[192,16384]{1,0:T(8,128)} %strain_ref.1, f32[128,128]{1,0:T(8,128)} %constant.10.clone.window_ref, bf16[256,256]{1,0:T(8,128)(2,1)} %constant.11.clone.first_ref, bf16[768,256]{1,0:T(8,128)(2,1)} %constant.12.clone.second_ref, ...), custom_call_target="tpu_custom_call" | custom-call | tf_op jit(solution)/shard_map/welch/pallas_call | solution.py:392
  110.0 2.1 %copy.12 = f32[192,1024]{1,0:T(8,128)} copy(f32[192,1024]{1,0:T(8,128)} %get-tuple-element.12) | data formatting | bytes 1572864
  112.1 1.2 %copy.13 = f32[192]{0:T(256)} copy(f32[192]{0:T(256)} %bitcast.4) | data formatting | bytes 1536
  113.3 1.3 %copy.14 = f32[1024]{0:T(1024)} copy(f32[1024]{0:T(1024)} %bitcast.3) | data formatting | bytes 8192

commit v4 on v3

--- a/solution.py
+++ b/solution.py
@@ -216,6 +216,63 @@
         def _():
             ref[...] = jnp.zeros_like(ref)
 
+    def chunk_of(m, side):
+        far = lax.rem(m, count - 1)
+        return far if side else count - 1 - far
+
+    def sum_part(m, side):
+        q = m // (count - 1)
+        return sums.at[pl.ds(chunk_of(m, side) * rows, rows), pl.ds(pl.multiple_of(q * width, ROWS), width)]
+
+    def edge_part(m, side):
+        return edge_sums.at[pl.ds(chunk_of(m, side) * rows, rows)]
+
+    def line(m, side):
+        target = (from_left, from_right)[side]
+        return pltpu.make_async_remote_copy(
+            src_ref=sum_part(m, side), dst_ref=target.at[m],
+            send_sem=line_send.at[side, m], recv_sem=line_recv.at[side, m],
+            device_id={"tm": me + (-1 if side else 1)}, device_id_type=pl.DeviceIdType.MESH,
+        )
+
+    def edge_line(m, side):
+        target = (edge_left, edge_right)[side]
+        far = lax.rem(m, count - 1)
+        return pltpu.make_async_remote_copy(
+            src_ref=edge_part(m, side), dst_ref=target.at[far],
+            send_sem=edge_send.at[side, far], recv_sem=edge_recv.at[side, far],
+            device_id={"tm": me + (-1 if side else 1)}, device_id_type=pl.DeviceIdType.MESH,
+        )
+
+    def take(m, side):
+        line(m, side).wait_recv()
+        part = sum_part(m, side)
+        part[...] = part[...] + (from_left, from_right)[side][m]
+
+        @pl.when(m >= (pieces - 1) * (count - 1))
+        def _():
+            edge_line(m, side).wait_recv()
+            edge = edge_part(m, side)
+            edge[...] = edge[...] + (edge_left, edge_right)[side][lax.rem(m, count - 1)]
+
+    messages = (count - 1) * pieces
+    hop = 2
+    early = max(1, count // 4)
+
+    def place_of(side):
+        return count - 1 - me if side else me
+
+    def take_and_send(m, side):
+        @pl.when(place_of(side) > 0)
+        def _():
+            take(m, side)
+
+        line(m, side).start()
+
+        @pl.when(m >= (pieces - 1) * (count - 1))
+        def _():
+            edge_line(m, side).start()
+
     @pl.loop(0, groups)
     def _(g):
         load(g, 0).wait()
@@ -237,77 +294,47 @@
             (window_ref, first_ref, second_ref, twist_ref), (buf, zbuf, ebuf, psum), put, put_edge,
         )
 
+        @pl.when(g == groups - 1)
+        def _():
+            for s in range(edge_sums.shape[1]):
+                edge_sums[:, s, :] = jnp.transpose(edge_rows[s * ROOT : (s + 1) * ROOT, :])
+
+        @pl.when(lax.rem(g + 1, groups // pieces) == 0)
+        def _():
+            q = g // (groups // pieces)
+            for side in range(2):
+                place = place_of(side)
+
+                @pl.when(place < early)
+                def _():
+                    @pl.loop(0, count - 1)
+                    def _(far):
+                        @pl.when(far < count - 1 - place)
+                        def _():
+                            take_and_send(q * (count - 1) + far, side)
+
     spread = edge_sums.shape[1]
-    for s in range(spread):
-        edge_sums[:, s, :] = jnp.transpose(edge_rows[s * ROOT : (s + 1) * ROOT, :])
-
-    def chunk_of(m, side):
-        far = m // pieces
-        return far if side else count - 1 - far
-
-    def sum_part(m, side):
-        q = lax.rem(m, pieces)
-        return sums.at[pl.ds(chunk_of(m, side) * rows, rows), pl.ds(pl.multiple_of(q * width, ROWS), width)]
-
-    def edge_part(m, side):
-        return edge_sums.at[pl.ds(chunk_of(m, side) * rows, rows)]
-
-    def line(m, side):
-        target = (from_left, from_right)[side]
-        return pltpu.make_async_remote_copy(
-            src_ref=sum_part(m, side), dst_ref=target.at[m],
-            send_sem=line_send.at[side, m], recv_sem=line_recv.at[side, m],
-            device_id={"tm": me + (-1 if side else 1)}, device_id_type=pl.DeviceIdType.MESH,
-        )
-
-    def edge_line(m, side):
-        target = (edge_left, edge_right)[side]
-        far = m // pieces
-        return pltpu.make_async_remote_copy(
-            src_ref=edge_part(m, side), dst_ref=target.at[far],
-            send_sem=edge_send.at[side, far], recv_sem=edge_recv.at[side, far],
-            device_id={"tm": me + (-1 if side else 1)}, device_id_type=pl.DeviceIdType.MESH,
-        )
-
-    def take(m, side):
-        line(m, side).wait_recv()
-        part = sum_part(m, side)
-        part[...] = part[...] + (from_left, from_right)[side][m]
-
-        @pl.when(lax.rem(m, pieces) == 0)
-        def _():
-            edge_line(m, side).wait_recv()
-            edge = edge_part(m, side)
-            edge[...] = edge[...] + (edge_left, edge_right)[side][m // pieces]
-
-    messages = (count - 1) * pieces
-
-    @pl.loop(0, messages + count - 1)
+
+    @pl.loop(0, messages + hop * (count - 1))
     def _(t):
         for side in range(2):
-            place = count - 1 - me if side else me
-            m = t - place
-
-            @pl.when(jnp.logical_and(m >= 0, m < (count - 1 - place) * pieces))
+            place = place_of(side)
+            m = t - hop * place
+
+            @pl.when(jnp.logical_and(place >= early, jnp.logical_and(m >= 0, m < messages)))
             def _():
-                @pl.when(place > 0)
+                @pl.when(lax.rem(m, count - 1) < count - 1 - place)
                 def _():
-                    take(m, side)
-
-                line(m, side).start()
-
-                @pl.when(lax.rem(m, pieces) == 0)
-                def _():
-                    edge_line(m, side).start()
+                    take_and_send(m, side)
 
     for side in range(2):
-        place = count - 1 - me if side else me
+        place = place_of(side)
 
         @pl.when(place > 0)
         def _():
             @pl.loop(0, pieces)
             def _(q):
-                take((count - 1 - place) * pieces + q, side)
+                take(q * (count - 1) + (count - 1 - place), side)
 
     nyquist_ref[...] = edge_sums[me * rows + per_dev] * scale
     for s in range(spread):
@@ -354,11 +381,11 @@
         for side in range(2):
             place = count - 1 - me if side else me
 
-            @pl.when(m < (count - 1 - place) * pieces)
+            @pl.when(lax.rem(m, count - 1) < count - 1 - place)
             def _():
                 line(m, side).wait_send()
 
-                @pl.when(lax.rem(m, pieces) == 0)
+                @pl.when(m >= (pieces - 1) * (count - 1))
                 def _():
                     edge_line(m, side).wait_send()
 

time: 115 us -> 109 us (0.948)
  the two profiles are of different devices: /device:TPU:8 before, /device:TPU:0 now
where the time goes in v4:
time: 109 us
  Pallas kernels  103 us (94%)
  local copies, waits for them, and re-layouts  4.57 us (4%)
    pallas_call x1, Pallas kernels, per_device(): pl.pallas_call(functools.partial(welch_kernel, pieces, 1.0 / (segments *...  103 us
    unnamed x3, local copies, waits for them, and re-layouts  4.57 us

profile of v4, /device:TPU:0, one launch (start us, length us, event | category | flops | bytes accessed | tf_op | source)
XLA Modules:
  0.0 108.6 jit_solution(8411850276691836737)
XLA Ops:
  0.6 103.4 %welch.1 = (f32[192,1024]{1,0:T(8,128)}, f32[2,128]{1,0:T(2,128)}, f32[8,128]{1,0:T(8,128)}) custom-call(f32[192,16384]{1,0:T(8,128)} %strain_ref.1, f32[128,128]{1,0:T(8,128)} %constant.10.clone.window_ref, bf16[256,256]{1,0:T(8,128)(2,1)} %constant.11.clone.first_ref, bf16[768,256]{1,0:T(8,128)(2,1)} %constant.12.clone.second_ref, ...), custom_call_target="tpu_custom_call" | custom-call | tf_op jit(solution)/shard_map/welch/pallas_call | solution.py:419
  104.0 2.1 %copy.12 = f32[192,1024]{1,0:T(8,128)} copy(f32[192,1024]{1,0:T(8,128)} %get-tuple-element.12) | data formatting | bytes 1572864
  106.1 1.2 %copy.13 = f32[192]{0:T(256)} copy(f32[192]{0:T(256)} %bitcast.4) | data formatting | bytes 1536
  107.3 1.3 %copy.14 = f32[1024]{0:T(1024)} copy(f32[1024]{0:T(1024)} %bitcast.3) | data formatting | bytes 8192
